TPU v7x, 256 devices: a whole 4x4x8 slice. The times are simulated.
256 devices in a mesh: row: 8 (over z), col: 32 (over x, y, core).
Axes of the slice: x: 4, y: 4, z: 8, core: 2. Of those that a mesh axis runs over, the one named last changes fastest.
Arguments:
- rho_real: float32 [4096, 4096], P('row', 'col'), may hold values from -2.5 to 4, as said below
- rho_imag: float32 [4096, 4096], P('row', 'col'), may hold values from -2.5 to 2.5, as said below
- hamiltonian: bfloat16 [4096, 4096], P('row', 'col'), may hold values from -1 to 1
- amplitudes: float32 [8, 4096], replicated, may hold values from 0.15 to 0.6
- offsets: int32 [8], replicated, may hold values from -16 to 16
- active_jumps: int32 [1], replicated, may hold values from 4 to 8
Outputs:
- rho_next_real: float32 [4096, 4096], P('row', 'col')
- rho_next_imag: float32 [4096, 4096], P('row', 'col')
Inputs may be any that keep to these rules, and one draw needn't show every extreme that they name: `rho_real`: symmetric, with every diagonal entry 0.5 or more. `rho_imag`: antisymmetric.
All inputs are finite; a program needn't handle non-finite values.
Results may differ from a plain program's by a relative error of at most 0.001.
Values may be sent and summed in bfloat16 or wider, within the bound.
A program may use at most 64 MiB of HBM per device.

v0:
```python
import jax
import jax.numpy as jnp
from jax import lax
from jax.sharding import Mesh
from jax.sharding import PartitionSpec as P

OMAX = 16
COL = ("col_0", "col_1", "col_2")
ROW_COL = ("row", "col_0", "col_1", "col_2")
step_size = 0.25


def in_order(tiles, dim):
    lengths = list(tiles.shape[1:])
    lengths[dim] *= tiles.shape[0]
    return jnp.moveaxis(tiles, 0, dim).reshape(lengths)


def sent_to_all(x, axis):
    peers = lax.axis_size(axis)
    return lax.all_to_all(jnp.broadcast_to(x[None], (peers, *x.shape)), axis, 0, 0, tiled=True)


def gathered_copies(x, axis, dim):
    return in_order(sent_to_all(x, axis), dim)


def by_axis(x, axes):
    for axis in axes:
        x = lax.psum(x, axis)
    return x


def in_one_piece(arrays, axis, dim, along):
    both = jnp.concatenate(arrays, axis=along)
    out, at, finished = (gathered_copies(both, axis, dim), 0, [])
    for a in arrays:
        finished.append(lax.slice_in_dim(out, at, at + a.shape[along], axis=along))
        at += a.shape[along]
    return tuple(finished)


def sent_together(arrays, axis, dim, along):
    both = jnp.concatenate(arrays, axis=along)
    out, at, finished = (lax.all_gather(both, axis, axis=dim, tiled=True), 0, [])
    for a in arrays:
        finished.append(lax.slice_in_dim(out, at, at + a.shape[along], axis=along))
        at += a.shape[along]
    return tuple(finished)


def extended(cells, sides, width):
    for axis, dim in sides:
        count = lax.axis_size(axis)
        ends = count - 1
        head = lax.slice_in_dim(cells, 0, width, axis=dim)
        tail = lax.slice_in_dim(cells, cells.shape[dim] - width, cells.shape[dim], axis=dim)
        cells = jnp.concatenate(
            [
                lax.ppermute(tail, axis, [(i, (i + 1) % count) for i in range(ends)]),
                cells,
                lax.ppermute(head, axis, [((i + 1) % count, i) for i in range(ends)]),
            ],
            axis=dim,
        )
    return cells


def dissipate(matrix, padded, amplitudes, offsets, active, row_first, col_first):
    height = matrix.shape[1]
    breadth = matrix.shape[2]
    levels = amplitudes.shape[1]
    margin = (padded.shape[1] - height) // 2
    positions = jnp.arange(levels, dtype=jnp.int32)
    summed = jnp.zeros(matrix.shape, matrix.dtype)
    for jump_slot in range(amplitudes.shape[0]):
        offset = offsets[jump_slot]
        inside = (positions + offset >= 0) & (positions + offset < levels)
        strength = jnp.where(inside, amplitudes[jump_slot], 0.0)
        outflow = jnp.pad(strength * strength, (margin, margin))
        outflow = lax.dynamic_slice_in_dim(outflow, margin - offset, levels)
        row_strength = lax.dynamic_slice_in_dim(strength, row_first, height)
        col_strength = lax.dynamic_slice_in_dim(strength, col_first, breadth)
        row_outflow = lax.dynamic_slice_in_dim(outflow, row_first, height)
        col_outflow = lax.dynamic_slice_in_dim(outflow, col_first, breadth)
        corner = margin + offset
        shifted = lax.dynamic_slice(padded, (jnp.int32(0), corner, corner), (2, height, breadth))
        contribution = (
            row_strength[:, None] * col_strength[None, :] * shifted
            - 0.5 * (row_outflow[:, None] + col_outflow[None, :]) * matrix
        )
        summed = summed + jnp.where(jump_slot < active, contribution, 0.0)
    return summed


def diagonal_sum(matrix, row_first, col_first):
    row_index = lax.broadcasted_iota(jnp.int32, matrix.shape, 0) + row_first
    col_index = lax.broadcasted_iota(jnp.int32, matrix.shape, 1) + col_first
    return jnp.sum(jnp.where(row_index == col_index, matrix, 0.0))


def local(rho_real, rho_imag, hamiltonian, amplitudes, offsets, active_jumps):
    height, breadth = rho_real.shape
    levels = amplitudes.shape[1]
    row_first = lax.axis_index("row") * height
    col_first = lax.axis_index(COL) * breadth
    active = active_jumps[0]
    ham_columns = gathered_copies(hamiltonian, "row", 0)
    start_trace = by_axis(diagonal_sum(rho_real, row_first, col_first), ROW_COL)

    def drift(real_part, imag_part):
        real_low = real_part.astype(jnp.bfloat16)
        imag_low = imag_part.astype(jnp.bfloat16)
        row_panel = lax.all_gather(hamiltonian, COL, axis=1, tiled=True)
        pieces = in_one_piece((real_low, imag_low), "row", 0, 1)
        strip = row_panel
        left_real = jnp.dot(strip, pieces[0], preferred_element_type=jnp.float32)
        left_imag = jnp.dot(strip, pieces[1], preferred_element_type=jnp.float32)
        pieces = sent_together((real_low, imag_low), COL, 1, 0)
        strip = ham_columns
        right_real = jnp.dot(pieces[0], strip, preferred_element_type=jnp.float32)
        right_imag = jnp.dot(pieces[1], strip, preferred_element_type=jnp.float32)
        matrix = jnp.stack([real_part, imag_part])
        padded = extended(matrix.astype(jnp.bfloat16), (("row", 1), (COL, 2)), OMAX).astype(
            matrix.dtype
        )
        loss = dissipate(matrix, padded, amplitudes, offsets, active, row_first, col_first)
        return (left_imag - right_imag + loss[0], right_real - left_real + loss[1])

    first_real, first_imag = drift(rho_real, rho_imag)
    middle_real = rho_real + step_size * first_real
    middle_imag = rho_imag + step_size * first_imag
    rescale = levels / start_trace
    middle_real = middle_real * rescale
    middle_imag = middle_imag * rescale
    second_real, second_imag = drift(middle_real, middle_imag)
    updated_real = rho_real + 0.5 * step_size * (first_real + second_real)
    updated_imag = rho_imag + 0.5 * step_size * (first_imag + second_imag)
    rescale = levels / start_trace
    return (updated_real * rescale, updated_imag * rescale)


def solution(mesh):
    split = Mesh(
        mesh.devices.reshape(mesh.shape["row"], 4, 4, 2), ("row", "col_0", "col_1", "col_2")
    )
    placed = (P("row", COL), P("row", COL), P("row", COL), P(), P(), P())
    return jax.shard_map(
        local,
        mesh=split,
        in_specs=placed,
        out_specs=(P("row", COL), P("row", COL)),
        check_vma=False,
    )
```

profile of v0, /device:TPU:25, one launch (start us, length us, event | category | flops | bytes accessed | tf_op | source)
XLA Modules:
  0.0 268.6 jit_solution(7100053074104402569)
XLA Ops:
  7.3 1.0 convert_element_type.42
  8.2 1.8 select_reduce_fusion
  10.0 0.7 pad_maximum_fusion.3
  10.8 0.7 all-gather.4.cloned.1.call-update
  11.5 1.1 copy.16
  12.6 1.1 copy.10
  13.7 0.7 fusion.83
  14.4 3.5 %collective-permute-start = (bf16[2,16,128]{1,2,0:T(8,128)(2,1)}, bf16[2,16,128]{1,2,0:T(8,128)(2,1)S(1)}, u32[]{:S(2)}, u32[]{:S(2)}) collective-permute-start(bf16[2,16,128]{1,2,0:T(8,128)(2,1)} %get-tuple-element.32), channel_id=1, source_target_pairs={{0,32},{32,64},{64,96},{96,128},{128,160},{160,192},{192,224},{1,3... | collective-permute-start | bytes 24584 | tf_op jit(solution)/shard_map/ppermute | solution.py:60
  18.0 1.3 collective-permute-start.1
  19.3 2.0 broadcast_in_dim.49
  21.3 9.8 %all-to-all-start.1 = ((bf16[8,512,128]{2,1,0:T(8,128)(2,1)}), bf16[8,512,128]{2,1,0:T(8,128)(2,1)S(1)}, u32[]{:S(2)}, u32[]{:S(2)}) async-start(bf16[8,512,128]{2,1,0:T(8,128)(2,1)} %broadcast_in_dim.49), calls=%async_computation.1 | async-start | bytes 2097152 | tf_op jit(solution)/shard_map/all_to_all | solution.py:21
  31.1 0.7 fusion.85
  34.6 0.6 fusion.76
  35.9 0.7 fusion.66
  37.1 0.7 fusion.70
  38.4 27.6 %psum.28 = f32[]{:T(128)} all-reduce(f32[]{:T(128)} %get-tuple-element.30), channel_id=1, replica_groups=mesh['row'=8,'col_0'=4,'col_1'=4,'col_2'=2] {'row'}, use_global_device_ids=true, to_apply=%region_1.2 | all-reduce | flops 1 | bytes 8 | tf_op jit(solution)/shard_map/psum | solution.py:30
  72.4 0.7 pad_dynamic-slice_fusion.8
  73.0 0.7 pad_dynamic-slice_fusion.10
  74.3 0.7 pad_dynamic-slice_fusion.12
  75.0 0.6 fusion.80
  76.2 0.7 pad_dynamic-slice_fusion.5
  76.9 0.7 pad_dynamic-slice_fusion.15
  77.5 0.7 pad_dynamic-slice_fusion.9
  79.4 1.5 broadcast_in_dim.48
  81.1 4.2 %all-to-all-start = ((bf16[8,512,256]{2,1,0:T(8,128)(2,1)}), bf16[8,512,256]{2,1,0:T(8,128)(2,1)S(1)}, u32[]{:S(2)}, u32[]{:S(2)}) async-start(bf16[8,512,256]{2,1,0:T(8,128)(2,1)} %broadcast_in_dim.48), calls=%async_computation | async-start | bytes 4194304 | tf_op jit(solution)/shard_map/all_to_all | solution.py:21
  85.9 9.1 %psum.29 = f32[]{:T(128)} all-reduce(f32[]{:T(128)} %psum.28), channel_id=1, replica_groups=mesh['row'=8,'col_0'=4,'col_1'=4,'col_2'=2] {'col_0'}, use_global_device_ids=true, to_apply=%region_2.3 | all-reduce | flops 1 | bytes 8 | tf_op jit(solution)/shard_map/psum | solution.py:30
  97.6 0.7 pad_dynamic-slice_fusion.7
  98.4 1.5 add_multiply_fusion.2
  99.9 0.9 broadcast_multiply_fusion.6
  100.8 1.6 add_multiply_fusion.8
  102.4 0.9 broadcast_multiply_fusion.4
  103.3 1.6 add_multiply_fusion.6
  104.9 0.9 broadcast_multiply_fusion.2
  106.4 6.6 %psum.30 = f32[]{:T(128)} all-reduce(f32[]{:T(128)} %psum.29), channel_id=1, replica_groups=mesh['row'=8,'col_0'=4,'col_1'=4,'col_2'=2] {'col_1'}, use_global_device_ids=true, to_apply=%region_3.4 | all-reduce | flops 1 | bytes 8 | tf_op jit(solution)/shard_map/psum | solution.py:30
  113.0 0.7 pad_maximum_fusion.11
  113.7 11.7 %collective-permute-start.2 = (bf16[2,544,16]{1,2,0:T(8,128)(2,1)}, bf16[2,544,16]{1,2,0:T(8,128)(2,1)}, u32[]{:S(2)}, u32[]{:S(2)}) collective-permute-start(bf16[2,544,16]{1,2,0:T(8,128)(2,1)} %get-tuple-element.26), channel_id=1, source_target_pairs={{0,1},{1,2},{2,3},{3,4},{4,5},{5,6},{6,7},{7,8},{8,9},{9,10},{10,1... | collective-permute-start | bytes 104456 | tf_op jit(solution)/shard_map/ppermute | solution.py:60
  125.4 1.9 collective-permute-start.3
  127.3 1.6 add_multiply_fusion.4
  128.9 3.2 %psum.31 = f32[]{:T(128)} all-reduce(f32[]{:T(128)} %psum.30), channel_id=1, replica_groups=mesh['row'=8,'col_0'=4,'col_1'=4,'col_2'=2] {'col_2'}, use_global_device_ids=true, to_apply=%region_4.5 | all-reduce | flops 1 | bytes 8 | tf_op jit(solution)/shard_map/psum | solution.py:30
  148.6 1.0 maximum_convert_fusion
  149.5 4.5 %select_add_fusion.1 = f32[2,512,128]{1,2,0:T(8,128)} fusion(f32[2,544,160]{1,2,0:T(8,128)S(1)} %maximum_convert_fusion, s32[]{:T(128)S(6)} %select_n.358, s32[]{:T(128)S(6)} %select_n.359, s32[]{:T(128)S(6)} %select_n.351, s32[]{:T(128)S(6)} %select_n.352, s32[]{:T(128)S(6)} %select_n.344, s32[]{:T(128)S(6)} %select_n.345, s32[]{:T(128)S(6)} %select_n.337, ...), kind=kLoop, calls=%fused_computation.35 | loop fusion | flops 5242880 | bytes 9437256 | tf_op jit(solution)/shard_map/add | solution.py:92
  154.1 4.0 %fusion.6 = f32[512,128]{0,1:T(8,128)S(1)} fusion(bf16[4096,128]{1,0:T(8,128)(2,1)} %bitcast.105, bf16[1024,4096]{1,0:T(8,128)(2,1)} %all-gather.6.cloned.1.call-done), kind=kOutput, calls=%fused_computation.6 | convolution fusion | flops 536870912 | bytes 5505024 | tf_op jit(solution)/shard_map/dot_general | solution.py:122
  158.1 3.8 %fusion.9 = f32[512,128]{0,1:T(8,128)S(1)} fusion(f32[512,128]{0,1:T(8,128)S(1)} %fusion.6, bf16[512,4096]{1,0:T(8,128)(2,1)} %all-gather.4.cloned.1.call-done, bf16[4096,256]{1,0:T(8,128)(2,1)S(1)} %bitcast.97, f32[2,512,128]{1,2,0:T(8,128)} %select_add_fusion.1), kind=kOutput, calls=%fused_computation.13 | convolution fusion | flops 537001984 | bytes 6029312 | tf_op jit(solution)/shard_map/dot_general | solution.py:118
  162.0 0.7 copy-done.5
  162.8 3.8 %fusion.4 = f32[512,128]{0,1:T(8,128)S(1)} fusion(bf16[4096,128]{1,0:T(8,128)(2,1)S(1)} %bitcast.108, bf16[1024,4096]{1,0:T(8,128)(2,1)} %all-gather.6.cloned.1.call-done), kind=kOutput, calls=%fused_computation.4 | convolution fusion | flops 536870912 | bytes 5505024 | tf_op jit(solution)/shard_map/dot_general | solution.py:121
  166.6 1.5 fusion.11
  168.2 0.7 copy-done.3
  168.9 0.7 pad_maximum_fusion.5
  169.9 1.4 broadcast_in_dim.53
  171.3 6.9 %all-to-all-start.2 = ((bf16[8,512,256]{2,1,0:T(8,128)(2,1)}), bf16[8,512,256]{2,1,0:T(8,128)(2,1)S(1)}, u32[]{:S(2)}, u32[]{:S(2)}) async-start(bf16[8,512,256]{2,1,0:T(8,128)(2,1)} %broadcast_in_dim.53), calls=%async_computation.2 | async-start | bytes 4194304 | tf_op jit(solution)/shard_map/all_to_all | solution.py:21
  178.3 3.4 %collective-permute-start.4 = (bf16[2,16,128]{1,2,0:T(8,128)(2,1)S(1)}, bf16[2,16,128]{1,2,0:T(8,128)(2,1)S(1)}, u32[]{:S(2)}, u32[]{:S(2)}) collective-permute-start(bf16[2,16,128]{1,2,0:T(8,128)(2,1)S(1)} %get-tuple-element.28), channel_id=1, source_target_pairs={{0,32},{32,64},{64,96},{96,128},{128,160},{160,192},{192,224},{1,3... | collective-permute-start | bytes 24584 | tf_op jit(solution)/shard_map/ppermute | solution.py:60
  181.7 1.3 collective-permute-start.5
  183.0 39.1 %collective-permute-done.4 = bf16[2,16,128]{1,2,0:T(8,128)(2,1)S(1)} collective-permute-done((bf16[2,16,128]{1,2,0:T(8,128)(2,1)S(1)}, bf16[2,16,128]{1,2,0:T(8,128)(2,1)S(1)}, u32[]{:S(2)}, u32[]{:S(2)}) %collective-permute-start.4) | collective-permute-done | bytes 8224 | tf_op jit(solution)/shard_map/ppermute | solution.py:60
  222.0 4.6 %collective-permute-done.5 = bf16[2,16,128]{1,2,0:T(8,128)(2,1)S(1)} collective-permute-done((bf16[2,16,128]{1,2,0:T(8,128)(2,1)S(1)}, bf16[2,16,128]{1,2,0:T(8,128)(2,1)S(1)}, u32[]{:S(2)}, u32[]{:S(2)}) %collective-permute-start.5) | collective-permute-done | bytes 8224 | tf_op jit(solution)/shard_map/ppermute | solution.py:62
  226.7 6.6 %collective-permute-start.6 = (bf16[2,544,16]{1,2,0:T(8,128)(2,1)S(1)}, bf16[2,544,16]{1,2,0:T(8,128)(2,1)S(1)}, u32[]{:S(2)}, u32[]{:S(2)}) collective-permute-start(bf16[2,544,16]{1,2,0:T(8,128)(2,1)S(1)} %get-tuple-element.24), channel_id=1, source_target_pairs={{0,1},{1,2},{2,3},{3,4},{4,5},{5,6},{6,7},{7,8},{8,9},{9,10},{10,1... | collective-permute-start | bytes 104456 | tf_op jit(solution)/shard_map/ppermute | solution.py:60
  233.3 2.1 collective-permute-start.7
  235.4 5.3 %collective-permute-done.7 = bf16[2,544,16]{1,2,0:T(8,128)(2,1)S(1)} collective-permute-done((bf16[2,544,16]{1,2,0:T(8,128)(2,1)S(1)}, bf16[2,544,16]{1,2,0:T(8,128)(2,1)S(1)}, u32[]{:S(2)}, u32[]{:S(2)}) %collective-permute-start.7) | collective-permute-done | bytes 34848 | tf_op jit(solution)/shard_map/ppermute | solution.py:62
  241.0 4.6 %select_add_fusion = f32[2,512,128]{1,2,0:T(8,128)} fusion(f32[2,544,160]{1,2,0:T(8,128)S(1)} %maximum_convert_fusion.1, s32[]{:T(128)S(6)} %select_n.358, s32[]{:T(128)S(6)} %select_n.359, s32[]{:T(128)S(6)} %select_n.351, s32[]{:T(128)S(6)} %select_n.352, s32[]{:T(128)S(6)} %select_n.344, s32[]{:T(128)S(6)} %select_n.345, s32[]{:T(128)S(6)} %select_n.337, ...), kind=kLoop, calls=%fused_computation.34 | loop fusion | flops 5242880 | bytes 9437256 | tf_op jit(solution)/shard_map/add | solution.py:92
  245.6 4.1 %fusion.2 = f32[512,128]{0,1:T(8,128)} fusion(bf16[4096,128]{1,0:T(8,128)(2,1)} %bitcast.106, bf16[1024,4096]{0,1:T(8,128)(2,1)} %all-gather.8.cloned.1.call-done), kind=kOutput, calls=%fused_computation.2 | convolution fusion | flops 536870912 | bytes 5505024 | tf_op jit(solution)/shard_map/dot_general | solution.py:122
  249.7 4.5 %fusion.17 = f32[512,128]{0,1:T(8,128)} fusion(f32[512,128]{0,1:T(8,128)S(1)} %copy.16, f32[512,128]{0,1:T(8,128)S(1)} %copy-done.6, f32[512,128]{0,1:T(8,128)} %fusion.2, bf16[512,4096]{1,0:T(8,128)(2,1)} %all-gather.4.cloned.1.call-done, bf16[4096,256]{1,0:T(8,128)(2,1)S(1)} %bitcast.99, f32[2,512,128]{1,2,0:T(8,128)S(1)} %copy-done.8, f32[]{:T(128)S(6)} %div.4), kind=kOutput, calls=%fused_computation.21 | convolution fusion | flops 537264128 | bytes 6553604 | tf_op jit(solution)/shard_map/dot_general | solution.py:118
  254.1 1.8 copy.19
  255.9 3.4 %fusion = f32[512,128]{0,1:T(8,128)S(1)} fusion(bf16[4096,128]{1,0:T(8,128)(2,1)} %bitcast.107, bf16[1024,4096]{0,1:T(8,128)(2,1)} %all-gather.8.cloned.1.call-done), kind=kOutput, calls=%fused_computation | convolution fusion | flops 536870912 | bytes 5505024 | tf_op jit(solution)/shard_map/dot_general | solution.py:121
  259.7 1.5 fusion.23
  261.3 0.8 copy.20
  (83 shorter events, 8.4 us)
Async XLA Ops:
  7.2 24.0 %copy-start.12 = (s32[8]{0:T(128)S(1)}, s32[8]{0:T(128)}, u32[]{:S(2)}) copy-start(s32[8]{0:T(128)} %param.10) | copy-start | bytes 100
  7.2 27.3 %copy-start.11 = (f32[8,4096]{1,0:T(8,128)S(1)}, f32[8,4096]{1,0:T(8,128)}, u32[]{:S(2)}) copy-start(f32[8,4096]{1,0:T(8,128)} %param.9) | copy-start | bytes 393220
  7.2 146.9 %all-gather.6.cloned.1.call-start = ((), (), s32[]{:S(2)}) async-start(), calls=%async_computation.4 | async-start | bytes 8650752 | tf_op jit(solution)/shard_map/all_gather | solution.py:45
  10.8 147.4 %all-gather.4.cloned.1.call-start = ((), (), s32[]{:S(2)}) async-start(), calls=%async_computation.3 | async-start | bytes 4325376 | tf_op jit(solution)/shard_map/all_gather | solution.py:114
  14.4 98.6 %collective-permute-start = (bf16[2,16,128]{1,2,0:T(8,128)(2,1)}, bf16[2,16,128]{1,2,0:T(8,128)(2,1)S(1)}, u32[]{:S(2)}, u32[]{:S(2)}) collective-permute-start(bf16[2,16,128]{1,2,0:T(8,128)(2,1)} %get-tuple-element.32), channel_id=1, source_target_pairs={{0,32},{32,64},{64,96},{96,128},{128,160},{160,192},{192,224},{1,3... | collective-permute-start | bytes 24584 | tf_op jit(solution)/shard_map/ppermute | solution.py:60
  18.0 95.0 %collective-permute-start.1 = (bf16[2,16,128]{1,2,0:T(8,128)(2,1)}, bf16[2,16,128]{1,2,0:T(8,128)(2,1)S(1)}, u32[]{:S(2)}, u32[]{:S(2)}) collective-permute-start(bf16[2,16,128]{1,2,0:T(8,128)(2,1)} %get-tuple-element.33), channel_id=1, source_target_pairs={{32,0},{64,32},{96,64},{128,96},{160,128},{192,160},{224,192},{33,... | collective-permute-start | bytes 24584 | tf_op jit(solution)/shard_map/ppermute | solution.py:62
  21.3 58.1 %all-to-all-start.1 = ((bf16[8,512,128]{2,1,0:T(8,128)(2,1)}), bf16[8,512,128]{2,1,0:T(8,128)(2,1)S(1)}, u32[]{:S(2)}, u32[]{:S(2)}) async-start(bf16[8,512,128]{2,1,0:T(8,128)(2,1)} %broadcast_in_dim.49), calls=%async_computation.1 | async-start | bytes 2097152 | tf_op jit(solution)/shard_map/all_to_all | solution.py:21
  79.4 1.6 copy-start.9
  81.1 77.0 %all-to-all-start = ((bf16[8,512,256]{2,1,0:T(8,128)(2,1)}), bf16[8,512,256]{2,1,0:T(8,128)(2,1)S(1)}, u32[]{:S(2)}, u32[]{:S(2)}) async-start(bf16[8,512,256]{2,1,0:T(8,128)(2,1)} %broadcast_in_dim.48), calls=%async_computation | async-start | bytes 4194304 | tf_op jit(solution)/shard_map/all_to_all | solution.py:21
  85.2 160.4 %all-gather.8.cloned.1.call-start = ((), (), s32[]{:S(2)}) async-start(), calls=%async_computation.5 | async-start | bytes 8650752 | tf_op jit(solution)/shard_map/all_gather | solution.py:45
  98.4 63.6 %copy-start.2 = (f32[512,128]{0,1:T(8,128)}, f32[512,128]{0,1:T(8,128)S(1)}, u32[]{:S(2)}) copy-start(f32[512,128]{0,1:T(8,128)S(1)} %get-tuple-element.59) | copy-start | bytes 786436
  113.7 34.8 %collective-permute-start.2 = (bf16[2,544,16]{1,2,0:T(8,128)(2,1)}, bf16[2,544,16]{1,2,0:T(8,128)(2,1)}, u32[]{:S(2)}, u32[]{:S(2)}) collective-permute-start(bf16[2,544,16]{1,2,0:T(8,128)(2,1)} %get-tuple-element.26), channel_id=1, source_target_pairs={{0,1},{1,2},{2,3},{3,4},{4,5},{5,6},{6,7},{7,8},{8,9},{9,10},{10,1... | collective-permute-start | bytes 104456 | tf_op jit(solution)/shard_map/ppermute | solution.py:60
  125.4 23.1 %collective-permute-start.3 = (bf16[2,544,16]{1,2,0:T(8,128)(2,1)}, bf16[2,544,16]{1,2,0:T(8,128)(2,1)}, u32[]{:S(2)}, u32[]{:S(2)}) collective-permute-start(bf16[2,544,16]{1,2,0:T(8,128)(2,1)} %get-tuple-element.27), channel_id=1, source_target_pairs={{1,0},{2,1},{3,2},{4,3},{5,4},{6,5},{7,6},{8,7},{9,8},{10,9},{11,1... | collective-permute-start | bytes 104456 | tf_op jit(solution)/shard_map/ppermute | solution.py:62
  158.1 4.6 %copy-start.10 = (bf16[8,512,128]{2,1,0:T(8,128)(2,1)S(1)}, bf16[8,512,128]{2,1,0:T(8,128)(2,1)}, u32[]{:S(2)}) copy-start(bf16[8,512,128]{2,1,0:T(8,128)(2,1)} %copy-done.9) | copy-start | bytes 3145732
  162.0 0.7 copy-start.5
  162.8 3.9 %copy-start = (bf16[512,4096]{1,0:T(8,128)(2,1)S(1)}, bf16[512,4096]{1,0:T(8,128)(2,1)}, u32[]{:S(2)}) copy-start(bf16[512,4096]{1,0:T(8,128)(2,1)} %all-gather.4.cloned.1.call-done) | copy-start | bytes 12582916
  162.8 3.9 %copy-start.7 = (f32[2,512,128]{1,2,0:T(8,128)S(1)}, f32[2,512,128]{1,2,0:T(8,128)}, u32[]{:S(2)}) copy-start(f32[2,512,128]{1,2,0:T(8,128)} %select_add_fusion.1) | copy-start | bytes 1572868
  168.2 0.7 copy-start.3
  171.3 78.4 %all-to-all-start.2 = ((bf16[8,512,256]{2,1,0:T(8,128)(2,1)}), bf16[8,512,256]{2,1,0:T(8,128)(2,1)S(1)}, u32[]{:S(2)}, u32[]{:S(2)}) async-start(bf16[8,512,256]{2,1,0:T(8,128)(2,1)} %broadcast_in_dim.53), calls=%async_computation.2 | async-start | bytes 4194304 | tf_op jit(solution)/shard_map/all_to_all | solution.py:21
  178.3 43.7 %collective-permute-start.4 = (bf16[2,16,128]{1,2,0:T(8,128)(2,1)S(1)}, bf16[2,16,128]{1,2,0:T(8,128)(2,1)S(1)}, u32[]{:S(2)}, u32[]{:S(2)}) collective-permute-start(bf16[2,16,128]{1,2,0:T(8,128)(2,1)S(1)} %get-tuple-element.28), channel_id=1, source_target_pairs={{0,32},{32,64},{64,96},{96,128},{128,160},{160,192},{192,224},{1,3... | collective-permute-start | bytes 24584 | tf_op jit(solution)/shard_map/ppermute | solution.py:60
  181.7 44.9 %collective-permute-start.5 = (bf16[2,16,128]{1,2,0:T(8,128)(2,1)S(1)}, bf16[2,16,128]{1,2,0:T(8,128)(2,1)S(1)}, u32[]{:S(2)}, u32[]{:S(2)}) collective-permute-start(bf16[2,16,128]{1,2,0:T(8,128)(2,1)S(1)} %get-tuple-element.29), channel_id=1, source_target_pairs={{32,0},{64,32},{96,64},{128,96},{160,128},{192,160},{224,192},{33,... | collective-permute-start | bytes 24584 | tf_op jit(solution)/shard_map/ppermute | solution.py:62
  226.7 8.7 %collective-permute-start.6 = (bf16[2,544,16]{1,2,0:T(8,128)(2,1)S(1)}, bf16[2,544,16]{1,2,0:T(8,128)(2,1)S(1)}, u32[]{:S(2)}, u32[]{:S(2)}) collective-permute-start(bf16[2,544,16]{1,2,0:T(8,128)(2,1)S(1)} %get-tuple-element.24), channel_id=1, source_target_pairs={{0,1},{1,2},{2,3},{3,4},{4,5},{5,6},{6,7},{7,8},{8,9},{9,10},{10,1... | collective-permute-start | bytes 104456 | tf_op jit(solution)/shard_map/ppermute | solution.py:60
  233.3 7.4 %collective-permute-start.7 = (bf16[2,544,16]{1,2,0:T(8,128)(2,1)S(1)}, bf16[2,544,16]{1,2,0:T(8,128)(2,1)S(1)}, u32[]{:S(2)}, u32[]{:S(2)}) collective-permute-start(bf16[2,544,16]{1,2,0:T(8,128)(2,1)S(1)} %get-tuple-element.25), channel_id=1, source_target_pairs={{1,0},{2,1},{3,2},{4,3},{5,4},{6,5},{7,6},{8,7},{9,8},{10,9},{11,1... | collective-permute-start | bytes 104456 | tf_op jit(solution)/shard_map/ppermute | solution.py:62
  245.6 4.1 %copy-start.6 = (f32[512,128]{0,1:T(8,128)S(1)}, f32[512,128]{0,1:T(8,128)}, u32[]{:S(2)}) copy-start(f32[512,128]{0,1:T(8,128)} %copy-done.5) | copy-start | bytes 786436
  245.6 4.1 %copy-start.8 = (f32[2,512,128]{1,2,0:T(8,128)S(1)}, f32[2,512,128]{1,2,0:T(8,128)}, u32[]{:S(2)}) copy-start(f32[2,512,128]{1,2,0:T(8,128)} %select_add_fusion) | copy-start | bytes 1572868
  255.9 3.8 %copy-start.1 = (bf16[512,4096]{1,0:T(8,128)(2,1)S(1)}, bf16[512,4096]{1,0:T(8,128)(2,1)}, u32[]{:S(2)}) copy-start(bf16[512,4096]{1,0:T(8,128)(2,1)} %all-gather.4.cloned.1.call-done) | copy-start | bytes 12582916
  255.9 3.8 %copy-start.4 = (f32[512,128]{0,1:T(8,128)S(1)}, f32[512,128]{0,1:T(8,128)}, u32[]{:S(2)}) copy-start(f32[512,128]{0,1:T(8,128)} %copy-done.3) | copy-start | bytes 786436
Sparse Core Ops, SparseCore 0:
  11.0 66.5 all-gather.5
  80.1 53.4 all-gather.3
  169.8 58.7 all-gather.7
where the time goes:
time: 270 us; the launch traced here: 269 us
  starting transfers between devices  52.8 us (20%)
  waiting for transfers between devices  49.7 us (18%)
  blocking collectives  46.5 us (17%)
  between operations  40.8 us (15%)
  other arithmetic  29.7 us (11%)
  matrix products  26.7 us (10%)
  local copies, waits for them, and re-layouts  22.4 us (8%)
    psum x4, blocking collectives, by_axis(): x = lax.psum(x, axis)  46.5 us
    ppermute x4, waiting for transfers between devices, extended(): lax.ppermute(tail, axis, [(i, (i + 1) % count) for i in range(ends)])  39.1 us
    ppermute x4, starting transfers between devices, extended(): lax.ppermute(tail, axis, [(i, (i + 1) % count) for i in range(ends)])  25.2 us
    all_to_all x3, starting transfers between devices, sent_to_all(): lax.all_to_all(jnp.broadcast_to(x[None], (peers, *x.shape)), axis, 0, 0,...  20.9 us
    ppermute x4, waiting for transfers between devices, extended(): lax.ppermute(head, axis, [((i + 1) % count, i) for i in range(ends)])  9.9 us
    add x2, other arithmetic, dissipate(): summed = summed + jnp.where(jump_slot < active, contribution, 0.0)  9.16 us
    dot_general x2, matrix products, drift(): left_imag = jnp.dot(strip, pieces[1], preferred_element_type=jnp.float32)  8.3 us
    dot_general x2, matrix products, drift(): right_imag = jnp.dot(pieces[1], strip, preferred_element_type=jnp.float32)  8.05 us
  transfers between devices with their start and end apart: 14, of which 3 were waited for; matrix products, arithmetic and copies ran while one was open for 19% of the time, Pallas kernels for 0%

commit v1 on v0

--- a/solution.py
+++ b/solution.py
@@ -27,7 +27,7 @@
 
 def by_axis(x, axes):
     for axis in axes:
-        x = lax.psum(x, axis)
+        x = jnp.sum(lax.all_gather(x, axis), axis=0)
     return x
 
 

time: 270 us -> 289 us (1.070)
  local copies, waits for them, and re-layouts: 22.4 us -> 40.6 us
  other arithmetic: 29.7 us -> 35.2 us
  blocking collectives: 46.5 us -> 42 us
    psum x4 -> x0, blocking collectives: 46.5 us -> none  [by_axis(): x = lax.psum(x, axis)]
    unnamed x0 -> x4, blocking collectives: none -> 42 us
    unnamed x30 -> x50, local copies, waits for them, and re-layouts: 6.65 us -> 15.9 us
    dynamic_slice x8, local copies, waits for them, and re-layouts: 0.59 us -> 5.15 us  [dissipate(): row_strength = lax.dynamic_slice_in_dim(strength, row_first, height)]
    dynamic_slice x8, local copies, waits for them, and re-layouts: 0.6 us -> 4.92 us  [dissipate(): col_strength = lax.dynamic_slice_in_dim(strength, col_first, breadth)]
  transfers between devices with their start and end apart: 14 -> 14, of which waited for: 3 -> 3; matrix products, arithmetic and copies ran while one was open for 19% -> 26% of each run, Pallas kernels for 0% -> 0%
where the time goes in v1:
time: 289 us; the launch traced here: 288 us
  starting transfers between devices  52.4 us (18%)
  waiting for transfers between devices  49.8 us (17%)
  blocking collectives  42 us (15%)
  between operations  41.2 us (14%)
  local copies, waits for them, and re-layouts  40.6 us (14%)
  other arithmetic  35.2 us (12%)
  matrix products  26.7 us (9%)
    unnamed x4, blocking collectives  42 us
    ppermute x4, waiting for transfers between devices, extended(): lax.ppermute(tail, axis, [(i, (i + 1) % count) for i in range(ends)])  39 us
    ppermute x4, starting transfers between devices, extended(): lax.ppermute(tail, axis, [(i, (i + 1) % count) for i in range(ends)])  24.8 us
    all_to_all x3, starting transfers between devices, sent_to_all(): lax.all_to_all(jnp.broadcast_to(x[None], (peers, *x.shape)), axis, 0, 0,...  20.9 us
    unnamed x50, local copies, waits for them, and re-layouts  15.9 us
    ppermute x4, waiting for transfers between devices, extended(): lax.ppermute(head, axis, [((i + 1) % count, i) for i in range(ends)])  9.92 us
    add x2, other arithmetic, dissipate(): summed = summed + jnp.where(jump_slot < active, contribution, 0.0)  9.19 us
    dot_general x2, matrix products, drift(): left_imag = jnp.dot(strip, pieces[1], preferred_element_type=jnp.float32)  8.3 us
  transfers between devices with their start and end apart: 14, of which 3 were waited for; matrix products, arithmetic and copies ran while one was open for 26% of the time, Pallas kernels for 0%

profile of v1, /device:TPU:25, one launch (start us, length us, event | category | flops | bytes accessed | tf_op | source)
XLA Modules:
  0.0 287.8 jit_solution(1842468939118752620)
XLA Ops:
  7.3 1.0 convert_element_type.42
  8.3 1.8 select_reduce_fusion
  10.0 0.7 pad_maximum_fusion.3
  10.8 0.7 all-gather.4.cloned.1.call-update
  11.5 1.1 copy.16
  12.6 1.1 copy.10
  13.7 0.7 fusion.83
  14.5 3.5 %collective-permute-start = (bf16[2,16,128]{1,2,0:T(8,128)(2,1)}, bf16[2,16,128]{1,2,0:T(8,128)(2,1)S(1)}, u32[]{:S(2)}, u32[]{:S(2)}) collective-permute-start(bf16[2,16,128]{1,2,0:T(8,128)(2,1)} %get-tuple-element.32), channel_id=1, source_target_pairs={{0,32},{32,64},{64,96},{96,128},{128,160},{160,192},{192,224},{1,3... | collective-permute-start | bytes 24584 | tf_op jit(solution)/shard_map/ppermute | solution.py:60
  18.0 1.3 collective-permute-start.1
  19.3 2.0 broadcast_in_dim.49
  21.3 9.8 %all-to-all-start.1 = ((bf16[8,512,128]{2,1,0:T(8,128)(2,1)}), bf16[8,512,128]{2,1,0:T(8,128)(2,1)S(1)}, u32[]{:S(2)}, u32[]{:S(2)}) async-start(bf16[8,512,128]{2,1,0:T(8,128)(2,1)} %broadcast_in_dim.49), calls=%async_computation.1 | async-start | bytes 2097152 | tf_op jit(solution)/shard_map/all_to_all | solution.py:21
  31.2 0.7 fusion.85
  34.5 0.7 dynamic-slice
  35.2 1.4 dynamic-update-slice
  38.0 0.7 fusion.66
  38.7 0.7 fusion.72
  40.7 25.0 %all-reduce.8 = f32[8]{0:T(128)S(1)} all-reduce(f32[8]{0:T(128)S(1)} %dynamic-update-slice), channel_id=1, replica_groups=mesh['row'=8,'col_0'=4,'col_1'=4,'col_2'=2] {'row'}, use_global_device_ids=true, to_apply=%add.8 | all-reduce | flops 8 | bytes 64
  73.2 1.4 dynamic-update-slice.1
  80.3 0.7 fusion.78
  81.7 1.5 broadcast_in_dim.48
  83.3 4.2 %all-to-all-start = ((bf16[8,512,256]{2,1,0:T(8,128)(2,1)}), bf16[8,512,256]{2,1,0:T(8,128)(2,1)S(1)}, u32[]{:S(2)}, u32[]{:S(2)}) async-start(bf16[8,512,256]{2,1,0:T(8,128)(2,1)} %broadcast_in_dim.48), calls=%async_computation | async-start | bytes 4194304 | tf_op jit(solution)/shard_map/all_to_all | solution.py:21
  88.1 8.3 %all-reduce.9 = f32[4]{0:T(128)S(1)} all-reduce(f32[4]{0:T(128)S(1)} %dynamic-update-slice.1), channel_id=1, replica_groups=mesh['row'=8,'col_0'=4,'col_1'=4,'col_2'=2] {'col_0'}, use_global_device_ids=true, to_apply=%add.9 | all-reduce | flops 4 | bytes 32
  109.1 1.5 dynamic-update-slice.2
  111.9 0.8 broadcast_multiply_fusion
  112.7 1.5 add_multiply_fusion.2
  114.2 1.6 broadcast_multiply_fusion.6
  115.8 1.6 add_multiply_fusion.8
  117.4 1.6 broadcast_multiply_fusion.4
  119.0 1.6 add_multiply_fusion.6
  120.6 1.6 broadcast_multiply_fusion.2
  122.8 6.2 %all-reduce.10 = f32[4]{0:T(128)S(1)} all-reduce(f32[4]{0:T(128)} %copy-done.16), channel_id=1, replica_groups=mesh['row'=8,'col_0'=4,'col_1'=4,'col_2'=2] {'col_1'}, use_global_device_ids=true, to_apply=%add.10 | all-reduce | flops 4 | bytes 32
  129.1 1.3 dynamic-slice.3
  131.0 1.3 dynamic-update-slice.3
  132.3 0.7 pad_maximum_fusion.11
  133.0 11.3 %collective-permute-start.2 = (bf16[2,544,16]{1,2,0:T(8,128)(2,1)}, bf16[2,544,16]{1,2,0:T(8,128)(2,1)}, u32[]{:S(2)}, u32[]{:S(2)}) collective-permute-start(bf16[2,544,16]{1,2,0:T(8,128)(2,1)} %get-tuple-element.26), channel_id=1, source_target_pairs={{0,1},{1,2},{2,3},{3,4},{4,5},{5,6},{6,7},{7,8},{8,9},{9,10},{10,1... | collective-permute-start | bytes 104456 | tf_op jit(solution)/shard_map/ppermute | solution.py:60
  144.3 1.9 collective-permute-start.3
  146.2 1.6 add_multiply_fusion.4
  147.8 2.5 all-reduce.11
  166.2 0.7 reduce_sum.49
  167.7 1.0 maximum_convert_fusion
  168.7 4.6 %select_add_fusion.1 = f32[2,512,128]{1,2,0:T(8,128)} fusion(f32[2,544,160]{1,2,0:T(8,128)S(1)} %maximum_convert_fusion, s32[]{:T(128)S(6)} %select_n.358, s32[]{:T(128)S(6)} %select_n.359, s32[]{:T(128)S(6)} %select_n.351, s32[]{:T(128)S(6)} %select_n.352, s32[]{:T(128)S(6)} %select_n.344, s32[]{:T(128)S(6)} %select_n.345, s32[]{:T(128)S(6)} %select_n.337, ...), kind=kLoop, calls=%fused_computation.35 | loop fusion | flops 5242880 | bytes 9437256 | tf_op jit(solution)/shard_map/add | solution.py:92
  173.2 4.0 %fusion.6 = f32[512,128]{0,1:T(8,128)S(1)} fusion(bf16[4096,128]{1,0:T(8,128)(2,1)} %bitcast.113, bf16[1024,4096]{1,0:T(8,128)(2,1)} %all-gather.6.cloned.1.call-done), kind=kOutput, calls=%fused_computation.6 | convolution fusion | flops 536870912 | bytes 5505024 | tf_op jit(solution)/shard_map/dot_general | solution.py:122
  177.3 3.8 %fusion.9 = f32[512,128]{0,1:T(8,128)S(1)} fusion(f32[512,128]{0,1:T(8,128)S(1)} %fusion.6, bf16[512,4096]{1,0:T(8,128)(2,1)} %all-gather.4.cloned.1.call-done, bf16[4096,256]{1,0:T(8,128)(2,1)S(1)} %bitcast.105, f32[2,512,128]{1,2,0:T(8,128)} %select_add_fusion.1), kind=kOutput, calls=%fused_computation.13 | convolution fusion | flops 537001984 | bytes 6029312 | tf_op jit(solution)/shard_map/dot_general | solution.py:118
  181.1 0.7 copy-done.5
  181.9 3.8 %fusion.4 = f32[512,128]{0,1:T(8,128)S(1)} fusion(bf16[4096,128]{1,0:T(8,128)(2,1)S(1)} %bitcast.116, bf16[1024,4096]{1,0:T(8,128)(2,1)} %all-gather.6.cloned.1.call-done), kind=kOutput, calls=%fused_computation.4 | convolution fusion | flops 536870912 | bytes 5505024 | tf_op jit(solution)/shard_map/dot_general | solution.py:121
  185.8 1.5 fusion.11
  187.3 0.7 copy-done.3
  188.0 0.7 pad_maximum_fusion.5
  189.0 1.4 broadcast_in_dim.53
  190.4 6.9 %all-to-all-start.2 = ((bf16[8,512,256]{2,1,0:T(8,128)(2,1)}), bf16[8,512,256]{2,1,0:T(8,128)(2,1)S(1)}, u32[]{:S(2)}, u32[]{:S(2)}) async-start(bf16[8,512,256]{2,1,0:T(8,128)(2,1)} %broadcast_in_dim.53), calls=%async_computation.2 | async-start | bytes 4194304 | tf_op jit(solution)/shard_map/all_to_all | solution.py:21
  197.4 3.4 %collective-permute-start.4 = (bf16[2,16,128]{1,2,0:T(8,128)(2,1)S(1)}, bf16[2,16,128]{1,2,0:T(8,128)(2,1)S(1)}, u32[]{:S(2)}, u32[]{:S(2)}) collective-permute-start(bf16[2,16,128]{1,2,0:T(8,128)(2,1)S(1)} %get-tuple-element.28), channel_id=1, source_target_pairs={{0,32},{32,64},{64,96},{96,128},{128,160},{160,192},{192,224},{1,3... | collective-permute-start | bytes 24584 | tf_op jit(solution)/shard_map/ppermute | solution.py:60
  200.8 1.3 collective-permute-start.5
  202.1 39.0 %collective-permute-done.4 = bf16[2,16,128]{1,2,0:T(8,128)(2,1)S(1)} collective-permute-done((bf16[2,16,128]{1,2,0:T(8,128)(2,1)S(1)}, bf16[2,16,128]{1,2,0:T(8,128)(2,1)S(1)}, u32[]{:S(2)}, u32[]{:S(2)}) %collective-permute-start.4) | collective-permute-done | bytes 8224 | tf_op jit(solution)/shard_map/ppermute | solution.py:60
  241.1 4.6 %collective-permute-done.5 = bf16[2,16,128]{1,2,0:T(8,128)(2,1)S(1)} collective-permute-done((bf16[2,16,128]{1,2,0:T(8,128)(2,1)S(1)}, bf16[2,16,128]{1,2,0:T(8,128)(2,1)S(1)}, u32[]{:S(2)}, u32[]{:S(2)}) %collective-permute-start.5) | collective-permute-done | bytes 8224 | tf_op jit(solution)/shard_map/ppermute | solution.py:62
  245.8 6.6 %collective-permute-start.6 = (bf16[2,544,16]{1,2,0:T(8,128)(2,1)S(1)}, bf16[2,544,16]{1,2,0:T(8,128)(2,1)S(1)}, u32[]{:S(2)}, u32[]{:S(2)}) collective-permute-start(bf16[2,544,16]{1,2,0:T(8,128)(2,1)S(1)} %get-tuple-element.24), channel_id=1, source_target_pairs={{0,1},{1,2},{2,3},{3,4},{4,5},{5,6},{6,7},{7,8},{8,9},{9,10},{10,1... | collective-permute-start | bytes 104456 | tf_op jit(solution)/shard_map/ppermute | solution.py:60
  252.4 2.1 collective-permute-start.7
  254.6 5.3 %collective-permute-done.7 = bf16[2,544,16]{1,2,0:T(8,128)(2,1)S(1)} collective-permute-done((bf16[2,544,16]{1,2,0:T(8,128)(2,1)S(1)}, bf16[2,544,16]{1,2,0:T(8,128)(2,1)S(1)}, u32[]{:S(2)}, u32[]{:S(2)}) %collective-permute-start.7) | collective-permute-done | bytes 34848 | tf_op jit(solution)/shard_map/ppermute | solution.py:62
  260.1 4.6 %select_add_fusion = f32[2,512,128]{1,2,0:T(8,128)} fusion(f32[2,544,160]{1,2,0:T(8,128)S(1)} %maximum_convert_fusion.1, s32[]{:T(128)S(6)} %select_n.358, s32[]{:T(128)S(6)} %select_n.359, s32[]{:T(128)S(6)} %select_n.351, s32[]{:T(128)S(6)} %select_n.352, s32[]{:T(128)S(6)} %select_n.344, s32[]{:T(128)S(6)} %select_n.345, s32[]{:T(128)S(6)} %select_n.337, ...), kind=kLoop, calls=%fused_computation.34 | loop fusion | flops 5242880 | bytes 9437256 | tf_op jit(solution)/shard_map/add | solution.py:92
  264.7 4.1 %fusion.2 = f32[512,128]{0,1:T(8,128)} fusion(bf16[4096,128]{1,0:T(8,128)(2,1)} %bitcast.114, bf16[1024,4096]{0,1:T(8,128)(2,1)} %all-gather.8.cloned.1.call-done), kind=kOutput, calls=%fused_computation.2 | convolution fusion | flops 536870912 | bytes 5505024 | tf_op jit(solution)/shard_map/dot_general | solution.py:122
  268.8 4.5 %fusion.17 = f32[512,128]{0,1:T(8,128)} fusion(f32[512,128]{0,1:T(8,128)S(1)} %copy.16, f32[512,128]{0,1:T(8,128)S(1)} %copy-done.6, f32[512,128]{0,1:T(8,128)} %fusion.2, bf16[512,4096]{1,0:T(8,128)(2,1)} %all-gather.4.cloned.1.call-done, bf16[4096,256]{1,0:T(8,128)(2,1)S(1)} %bitcast.107, f32[2,512,128]{1,2,0:T(8,128)S(1)} %copy-done.8, f32[]{:T(128)S(6)} %div.4), kind=kOutput, calls=%fused_computation.21 | convolution fusion | flops 537264128 | bytes 6553604 | tf_op jit(solution)/shard_map/dot_general | solution.py:118
  273.3 1.8 copy.19
  275.1 3.4 %fusion = f32[512,128]{0,1:T(8,128)S(1)} fusion(bf16[4096,128]{1,0:T(8,128)(2,1)} %bitcast.115, bf16[1024,4096]{0,1:T(8,128)(2,1)} %all-gather.8.cloned.1.call-done), kind=kOutput, calls=%fused_computation | convolution fusion | flops 536870912 | bytes 5505024 | tf_op jit(solution)/shard_map/dot_general | solution.py:121
  278.8 1.5 fusion.23
  280.4 0.8 copy.20
  (107 shorter events, 26.0 us)
Async XLA Ops:
  7.2 27.3 %copy-start.15 = (u32[256]{0:T(256)S(1)}, u32[256]{0:T(256)}, u32[]{:S(2)}) copy-start(u32[256]{0:T(256)} %constant.180) | copy-start | bytes 3076
  7.2 64.7 %copy-start.14 = (u32[256]{0:T(256)S(1)}, u32[256]{0:T(256)}, u32[]{:S(2)}) copy-start(u32[256]{0:T(256)} %constant.185) | copy-start | bytes 3076
  7.2 24.0 %copy-start.12 = (s32[8]{0:T(128)S(1)}, s32[8]{0:T(128)}, u32[]{:S(2)}) copy-start(s32[8]{0:T(128)} %param.10) | copy-start | bytes 100
  7.2 29.4 %copy-start.11 = (f32[8,4096]{1,0:T(8,128)S(1)}, f32[8,4096]{1,0:T(8,128)}, u32[]{:S(2)}) copy-start(f32[8,4096]{1,0:T(8,128)} %param.9) | copy-start | bytes 393220
  7.2 166.0 %all-gather.6.cloned.1.call-start = ((), (), s32[]{:S(2)}) async-start(), calls=%async_computation.4 | async-start | bytes 8650752 | tf_op jit(solution)/shard_map/all_gather | solution.py:45
  10.8 166.5 %all-gather.4.cloned.1.call-start = ((), (), s32[]{:S(2)}) async-start(), calls=%async_computation.3 | async-start | bytes 4325376 | tf_op jit(solution)/shard_map/all_gather | solution.py:114
  14.5 117.8 %collective-permute-start = (bf16[2,16,128]{1,2,0:T(8,128)(2,1)}, bf16[2,16,128]{1,2,0:T(8,128)(2,1)S(1)}, u32[]{:S(2)}, u32[]{:S(2)}) collective-permute-start(bf16[2,16,128]{1,2,0:T(8,128)(2,1)} %get-tuple-element.32), channel_id=1, source_target_pairs={{0,32},{32,64},{64,96},{96,128},{128,160},{160,192},{192,224},{1,3... | collective-permute-start | bytes 24584 | tf_op jit(solution)/shard_map/ppermute | solution.py:60
  18.0 114.3 %collective-permute-start.1 = (bf16[2,16,128]{1,2,0:T(8,128)(2,1)}, bf16[2,16,128]{1,2,0:T(8,128)(2,1)S(1)}, u32[]{:S(2)}, u32[]{:S(2)}) collective-permute-start(bf16[2,16,128]{1,2,0:T(8,128)(2,1)} %get-tuple-element.33), channel_id=1, source_target_pairs={{32,0},{64,32},{96,64},{128,96},{160,128},{192,160},{224,192},{33,... | collective-permute-start | bytes 24584 | tf_op jit(solution)/shard_map/ppermute | solution.py:62
  21.3 60.4 %all-to-all-start.1 = ((bf16[8,512,128]{2,1,0:T(8,128)(2,1)}), bf16[8,512,128]{2,1,0:T(8,128)(2,1)S(1)}, u32[]{:S(2)}, u32[]{:S(2)}) async-start(bf16[8,512,128]{2,1,0:T(8,128)(2,1)} %broadcast_in_dim.49), calls=%async_computation.1 | async-start | bytes 2097152 | tf_op jit(solution)/shard_map/all_to_all | solution.py:21
  31.2 76.6 %copy-start.13 = (u32[256]{0:T(256)S(1)}, u32[256]{0:T(256)}, u32[]{:S(2)}) copy-start(u32[256]{0:T(256)} %constant.190) | copy-start | bytes 3076
  81.7 1.6 copy-start.9
  83.3 93.9 %all-to-all-start = ((bf16[8,512,256]{2,1,0:T(8,128)(2,1)}), bf16[8,512,256]{2,1,0:T(8,128)(2,1)S(1)}, u32[]{:S(2)}, u32[]{:S(2)}) async-start(bf16[8,512,256]{2,1,0:T(8,128)(2,1)} %broadcast_in_dim.48), calls=%async_computation | async-start | bytes 4194304 | tf_op jit(solution)/shard_map/all_to_all | solution.py:21
  87.5 177.2 %all-gather.8.cloned.1.call-start = ((), (), s32[]{:S(2)}) async-start(), calls=%async_computation.5 | async-start | bytes 8650752 | tf_op jit(solution)/shard_map/all_gather | solution.py:45
  110.6 0.6 copy-start.16
  112.7 68.4 %copy-start.2 = (f32[512,128]{0,1:T(8,128)}, f32[512,128]{0,1:T(8,128)S(1)}, u32[]{:S(2)}) copy-start(f32[512,128]{0,1:T(8,128)S(1)} %get-tuple-element.59) | copy-start | bytes 786436
  133.0 34.6 %collective-permute-start.2 = (bf16[2,544,16]{1,2,0:T(8,128)(2,1)}, bf16[2,544,16]{1,2,0:T(8,128)(2,1)}, u32[]{:S(2)}, u32[]{:S(2)}) collective-permute-start(bf16[2,544,16]{1,2,0:T(8,128)(2,1)} %get-tuple-element.26), channel_id=1, source_target_pairs={{0,1},{1,2},{2,3},{3,4},{4,5},{5,6},{6,7},{7,8},{8,9},{9,10},{10,1... | collective-permute-start | bytes 104456 | tf_op jit(solution)/shard_map/ppermute | solution.py:60
  144.3 23.4 %collective-permute-start.3 = (bf16[2,544,16]{1,2,0:T(8,128)(2,1)}, bf16[2,544,16]{1,2,0:T(8,128)(2,1)}, u32[]{:S(2)}, u32[]{:S(2)}) collective-permute-start(bf16[2,544,16]{1,2,0:T(8,128)(2,1)} %get-tuple-element.27), channel_id=1, source_target_pairs={{1,0},{2,1},{3,2},{4,3},{5,4},{6,5},{7,6},{8,7},{9,8},{10,9},{11,1... | collective-permute-start | bytes 104456 | tf_op jit(solution)/shard_map/ppermute | solution.py:62
  177.3 4.6 %copy-start.10 = (bf16[8,512,128]{2,1,0:T(8,128)(2,1)S(1)}, bf16[8,512,128]{2,1,0:T(8,128)(2,1)}, u32[]{:S(2)}) copy-start(bf16[8,512,128]{2,1,0:T(8,128)(2,1)} %copy-done.9) | copy-start | bytes 3145732
  181.1 0.7 copy-start.5
  181.9 3.9 %copy-start = (bf16[512,4096]{1,0:T(8,128)(2,1)S(1)}, bf16[512,4096]{1,0:T(8,128)(2,1)}, u32[]{:S(2)}) copy-start(bf16[512,4096]{1,0:T(8,128)(2,1)} %all-gather.4.cloned.1.call-done) | copy-start | bytes 12582916
  181.9 3.9 %copy-start.7 = (f32[2,512,128]{1,2,0:T(8,128)S(1)}, f32[2,512,128]{1,2,0:T(8,128)}, u32[]{:S(2)}) copy-start(f32[2,512,128]{1,2,0:T(8,128)} %select_add_fusion.1) | copy-start | bytes 1572868
  187.3 0.7 copy-start.3
  190.4 78.4 %all-to-all-start.2 = ((bf16[8,512,256]{2,1,0:T(8,128)(2,1)}), bf16[8,512,256]{2,1,0:T(8,128)(2,1)S(1)}, u32[]{:S(2)}, u32[]{:S(2)}) async-start(bf16[8,512,256]{2,1,0:T(8,128)(2,1)} %broadcast_in_dim.53), calls=%async_computation.2 | async-start | bytes 4194304 | tf_op jit(solution)/shard_map/all_to_all | solution.py:21
  197.4 43.7 %collective-permute-start.4 = (bf16[2,16,128]{1,2,0:T(8,128)(2,1)S(1)}, bf16[2,16,128]{1,2,0:T(8,128)(2,1)S(1)}, u32[]{:S(2)}, u32[]{:S(2)}) collective-permute-start(bf16[2,16,128]{1,2,0:T(8,128)(2,1)S(1)} %get-tuple-element.28), channel_id=1, source_target_pairs={{0,32},{32,64},{64,96},{96,128},{128,160},{160,192},{192,224},{1,3... | collective-permute-start | bytes 24584 | tf_op jit(solution)/shard_map/ppermute | solution.py:60
  200.8 44.9 %collective-permute-start.5 = (bf16[2,16,128]{1,2,0:T(8,128)(2,1)S(1)}, bf16[2,16,128]{1,2,0:T(8,128)(2,1)S(1)}, u32[]{:S(2)}, u32[]{:S(2)}) collective-permute-start(bf16[2,16,128]{1,2,0:T(8,128)(2,1)S(1)} %get-tuple-element.29), channel_id=1, source_target_pairs={{32,0},{64,32},{96,64},{128,96},{160,128},{192,160},{224,192},{33,... | collective-permute-start | bytes 24584 | tf_op jit(solution)/shard_map/ppermute | solution.py:62
  245.8 8.7 %collective-permute-start.6 = (bf16[2,544,16]{1,2,0:T(8,128)(2,1)S(1)}, bf16[2,544,16]{1,2,0:T(8,128)(2,1)S(1)}, u32[]{:S(2)}, u32[]{:S(2)}) collective-permute-start(bf16[2,544,16]{1,2,0:T(8,128)(2,1)S(1)} %get-tuple-element.24), channel_id=1, source_target_pairs={{0,1},{1,2},{2,3},{3,4},{4,5},{5,6},{6,7},{7,8},{8,9},{9,10},{10,1... | collective-permute-start | bytes 104456 | tf_op jit(solution)/shard_map/ppermute | solution.py:60
  252.4 7.4 %collective-permute-start.7 = (bf16[2,544,16]{1,2,0:T(8,128)(2,1)S(1)}, bf16[2,544,16]{1,2,0:T(8,128)(2,1)S(1)}, u32[]{:S(2)}, u32[]{:S(2)}) collective-permute-start(bf16[2,544,16]{1,2,0:T(8,128)(2,1)S(1)} %get-tuple-element.25), channel_id=1, source_target_pairs={{1,0},{2,1},{3,2},{4,3},{5,4},{6,5},{7,6},{8,7},{9,8},{10,9},{11,1... | collective-permute-start | bytes 104456 | tf_op jit(solution)/shard_map/ppermute | solution.py:62
  264.7 4.1 %copy-start.6 = (f32[512,128]{0,1:T(8,128)S(1)}, f32[512,128]{0,1:T(8,128)}, u32[]{:S(2)}) copy-start(f32[512,128]{0,1:T(8,128)} %copy-done.5) | copy-start | bytes 786436
  264.7 4.1 %copy-start.8 = (f32[2,512,128]{1,2,0:T(8,128)S(1)}, f32[2,512,128]{1,2,0:T(8,128)}, u32[]{:S(2)}) copy-start(f32[2,512,128]{1,2,0:T(8,128)} %select_add_fusion) | copy-start | bytes 1572868
  275.1 3.8 %copy-start.1 = (bf16[512,4096]{1,0:T(8,128)(2,1)S(1)}, bf16[512,4096]{1,0:T(8,128)(2,1)}, u32[]{:S(2)}) copy-start(bf16[512,4096]{1,0:T(8,128)(2,1)} %all-gather.4.cloned.1.call-done) | copy-start | bytes 12582916
  275.1 3.8 %copy-start.4 = (f32[512,128]{0,1:T(8,128)S(1)}, f32[512,128]{0,1:T(8,128)}, u32[]{:S(2)}) copy-start(f32[512,128]{0,1:T(8,128)} %copy-done.3) | copy-start | bytes 786436
Sparse Core Ops, SparseCore 0:
  11.1 66.5 all-gather.5
  80.1 53.4 all-gather.3
  188.9 58.7 all-gather.7
